TPU v7x, 32 devices: a whole 2x2x4 slice. The times are simulated.
32 devices in a mesh: grp: 4 (over y, x), chan: 8 (over z, core).
Axes of the slice: x: 2, y: 2, z: 4, core: 2. Of those that a mesh axis runs over, the one named last changes fastest.
Arguments:
- visibility: float32 [1024, 32768], P('chan', 'grp'), may hold values from -6 to 6
- interference_mask: int32 [1024, 16384], P(None, ('grp', 'chan')), may hold values from 0 to 1
- valid_time_count: int32 [512], P(('grp', 'chan')), may hold values from 8 to 32
- fit_modes: float32 [1024, 32], P('grp'), may hold values from -1 to 1
Outputs:
- residual_vis: float32 [1024, 32768], P('chan', 'grp')
All inputs are finite; a program needn't handle non-finite values.
Results may differ from a plain program's by a relative error of at most 0.0003.
Values sent between devices are 32-bit elements; how exact they have to be, the bound alone decides.
A program may use at most 128 MiB of HBM per device.

v0:
```python
import jax
import jax.numpy as jnp
from jax import lax
from jax.sharding import PartitionSpec as P

damping = 0.1


def fit_weight(interference_mask, valid_time_count):
    antenna_pairs_list = valid_time_count.shape[0]
    sample_values = interference_mask.shape[1] // antenna_pairs_list
    projection_sums = lax.broadcasted_iota(jnp.int32, (antenna_pairs_list, sample_values), 1)
    within_range = (
        (projection_sums < valid_time_count[:, None])
        .astype(jnp.float32)
        .reshape(1, antenna_pairs_list * sample_values)
    )
    return (1.0 - interference_mask.astype(jnp.float32)) * within_range


def solve_normal(normal_matrix, target_signal):
    span_length = normal_matrix.shape[0]
    trailing = normal_matrix
    columns = []
    for position in range(span_length):
        column = trailing[:, 0] / jnp.sqrt(trailing[0, 0])
        columns.append(column)
        trailing = trailing[1:, 1:] - column[1:, None, :] * column[None, 1:, :]
    remains = target_signal
    forward = []
    for position in range(span_length):
        column = columns[position]
        current = remains[0] / column[0][None, :]
        forward.append(current)
        remains = remains[1:] - column[1:, None, :] * current[None]
    solution_values = [None] * span_length
    for position in reversed(range(span_length)):
        column = columns[position]
        current = forward[position]
        if position + 1 < span_length:
            later_rows = jnp.stack(solution_values[position + 1 :], 0)
            current = current - jnp.sum(column[1:, None, :] * later_rows, axis=0)
        solution_values[position] = current / column[0][None, :]
    return jnp.stack(solution_values, 0)


def solve_amplitudes(spectral_templates, assigned_rows, sample_weight, antenna_pairs_list):
    channel_count, span_length = spectral_templates.shape
    sample_values = sample_weight.shape[1] // antenna_pairs_list
    pairs = (spectral_templates[:, :, None] * spectral_templates[:, None, :]).reshape(
        channel_count, span_length * span_length
    )
    normal_matrix = lax.dot_general(
        pairs,
        sample_weight,
        (((0,), (0,)), ((), ())),
        precision=lax.Precision.HIGHEST,
        preferred_element_type=jnp.float32,
    )
    normal_matrix = normal_matrix.reshape(
        span_length, span_length, antenna_pairs_list * sample_values
    )
    normal_matrix = (
        normal_matrix + damping * jnp.eye(span_length, dtype=normal_matrix.dtype)[:, :, None]
    )
    weighted_values = assigned_rows.reshape(
        channel_count, antenna_pairs_list, 2, sample_values
    ) * sample_weight.reshape(channel_count, antenna_pairs_list, 1, sample_values)
    weighted_values = weighted_values.reshape(channel_count, antenna_pairs_list * 2 * sample_values)
    template_projection = lax.dot_general(
        spectral_templates,
        weighted_values,
        (((0,), (0,)), ((), ())),
        precision=lax.Precision.HIGHEST,
        preferred_element_type=jnp.float32,
    )
    target_signal = (
        template_projection.reshape(span_length, antenna_pairs_list, 2, sample_values)
        .transpose(0, 2, 1, 3)
        .reshape(span_length, 2, antenna_pairs_list * sample_values)
    )
    solution_values = solve_normal(normal_matrix, target_signal)
    return (
        solution_values.reshape(span_length, 2, antenna_pairs_list, sample_values)
        .transpose(0, 2, 1, 3)
        .reshape(span_length, antenna_pairs_list * 2 * sample_values)
    )


def per_device(visibility, interference_mask, valid_time_count, fit_modes):
    spectral_templates = lax.all_gather(fit_modes, "grp", axis=0, tiled=True)
    assigned_rows = lax.all_to_all(visibility, "chan", split_axis=1, concat_axis=0, tiled=True)
    antenna_pairs_list = valid_time_count.shape[0]
    sample_weight = fit_weight(interference_mask, valid_time_count)
    mode_amplitudes = solve_amplitudes(
        spectral_templates, assigned_rows, sample_weight, antenna_pairs_list
    )
    local_rows = visibility.shape[0]
    local_basis = lax.dynamic_slice_in_dim(
        spectral_templates, lax.axis_index("chan") * local_rows, local_rows, 0
    )
    model = jnp.dot(
        local_basis,
        lax.all_gather(mode_amplitudes, "chan", axis=1, tiled=True),
        precision=lax.Precision.HIGHEST,
        preferred_element_type=jnp.float32,
    )
    return visibility - model


def solution(mesh):
    placed = (P("chan", "grp"), P(None, ("grp", "chan")), P(("grp", "chan")), P("grp", None))
    return jax.shard_map(
        per_device, mesh=mesh, in_specs=placed, out_specs=P("chan", "grp"), check_vma=False
    )
```

profile of v0, /device:TPU:0, one launch (start us, length us, event | category | flops | bytes accessed | tf_op | source)
XLA Modules:
  0.0 204.1 jit_solution(10742631934232733337)
XLA Ops:
  6.5 5.6 %copy.41 = f32[128,8192]{0,1:T(8,128)} copy(f32[128,8192]{1,0:T(8,128)} %param.4) | data formatting | bytes 8388608 | tf_op args[0]
  12.1 6.5 %all-to-all-start = ((f32[128,8,1024]{0,2,1:T(8,128)}), f32[128,8,1024]{0,2,1:T(8,128)}, u32[]{:S(2)}, u32[]{:S(2)}) async-start(f32[128,8,1024]{0,2,1:T(8,128)} %bitcast.362), calls=%async_computation | async-start | bytes 8388608 | tf_op jit(solution)/shard_map/all_to_all | solution.py:92
  18.8 8.5 %all_gather.6 = f32[1024,32]{0,1:T(8,128)S(1)} all-gather(f32[256,32]{0,1:T(8,128)S(1)} %copy-done.17), channel_id=1, replica_groups=mesh['grp'=4,'chan'=8] {'grp'}, dimensions={0}, use_global_device_ids=true | all-gather | bytes 163840 | tf_op jit(solution)/shard_map/all_gather | solution.py:91
  27.3 1.8 copy.43
  29.1 1.8 subtract_multiply_fusion
  30.9 6.7 %fusion.6 = f32[32,32,512]{2,1,0:T(8,128)S(1)} fusion(f32[1024,512]{0,1:T(8,128)S(1)} %subtract_multiply_fusion, f32[1024,32]{0,1:T(8,128)S(1)} %all_gather.6, f32[32,32]{1,0:T(8,128)S(1)} %fusion.13), kind=kOutput, calls=%fused_computation.16 | convolution fusion | flops 6444023808 | bytes 4329472 | tf_op jit(solution)/shard_map/dot_general | solution.py:53
  52.8 0.7 div.867
  53.5 2.5 %mul.536 = f32[1024,16,2,32]{0,3,2,1:T(8,128)} broadcast(f32[1024,16,32]{0,2,1:T(8,128)S(1)} %bitcast.364), dimensions={0,1,3} | broadcast | bytes 6291456 | tf_op jit(solution)/shard_map/mul | solution.py:66
  56.0 5.3 %copy.44 = f32[1024,1024]{1,0:T(8,128)} copy(f32[1024,1024]{0,1:T(8,128)} %bitcast.363) | data formatting | bytes 8388608 | tf_op jit(solution)/shard_map/mul | solution.py:66
  61.4 51.3 %all-to-all-done = f32[128,8,1024]{0,2,1:T(8,128)} async-done(((f32[128,8,1024]{0,2,1:T(8,128)}), f32[128,8,1024]{0,2,1:T(8,128)}, u32[]{:S(2)}, u32[]{:S(2)}) %all-to-all-start) | async-done | bytes 4194336 | tf_op jit(solution)/shard_map/all_to_all | solution.py:92
  112.7 5.3 %copy.42 = f32[8,128,1024]{2,1,0:T(8,128)} copy(f32[8,128,1024]{1,2,0:T(8,128)} %bitcast.1) | data formatting | bytes 8388608 | tf_op jit(solution)/shard_map/all_to_all | solution.py:92
  118.0 4.4 %bitcast_multiply_fusion = f32[1024,1024]{1,0:T(8,128)S(1)} fusion(f32[1024,1024]{1,0:T(8,128)} %copy.44, f32[8,128,1024]{2,1,0:T(8,128)} %copy.42), kind=kLoop, calls=%fused_computation.3 | loop fusion | flops 1048576 | bytes 12582912 | tf_op jit(solution)/shard_map/mul | solution.py:66
  122.4 2.6 %convolution_bitcast_fusion = f32[32,1024]{1,0:T(8,128)S(1)} fusion(f32[1024,1024]{1,0:T(8,128)S(1)} %bitcast_multiply_fusion, f32[1024,32]{0,1:T(8,128)S(1)} %all_gather.6), kind=kOutput, calls=%fused_computation.18 | convolution fusion | flops 402653184 | bytes 4456448 | tf_op jit(solution)/shard_map/dot_general | solution.py:70
  128.3 0.7 slice_subtract_fusion.58
  129.2 0.7 stack.184
  129.9 0.7 stack.183
  130.6 0.7 fusion.46
  131.4 0.7 stack.182
  132.0 0.7 fusion.45
  132.8 0.7 constant_dynamic-update-slice_fusion.4
  133.6 1.3 constant_dynamic-update-slice_fusion.10
  136.1 0.6 constant_dynamic-update-slice_fusion.7
  137.9 0.8 multiply_reduce_fusion.25
  138.7 1.3 constant_dynamic-update-slice_fusion.17
  140.0 0.7 stack.179
  141.8 0.6 constant_dynamic-update-slice_fusion.14
  144.2 0.8 multiply_reduce_fusion.24
  145.0 0.7 constant_dynamic-update-slice_fusion.25
  145.7 0.7 stack.178
  146.4 0.7 constant_dynamic-update-slice_fusion.34
  147.1 0.7 stack.177
  147.9 0.7 constant_dynamic-update-slice_fusion.44
  148.8 0.7 constant_dynamic-update-slice_fusion.55
  149.7 0.7 constant_dynamic-update-slice_fusion.67
  150.7 0.7 constant_dynamic-update-slice_fusion.80
  151.6 0.7 constant_dynamic-update-slice_fusion.94
  152.6 0.7 constant_dynamic-update-slice_fusion.109
  153.8 0.7 constant_dynamic-update-slice_fusion.142
  154.9 0.7 constant_dynamic-update-slice_fusion.160
  155.9 0.7 constant_dynamic-update-slice_fusion.179
  156.9 0.6 constant_dynamic-update-slice_fusion.199
  157.9 0.6 constant_dynamic-update-slice_fusion.220
  158.9 0.7 constant_dynamic-update-slice_fusion.242
  160.0 0.6 constant_dynamic-update-slice_fusion.265
  161.0 0.6 constant_dynamic-update-slice_fusion.289
  166.6 1.3 reshape.1023
  167.9 21.3 %all-gather.2.cloned.1.call-done = f32[32,8192]{1,0:T(8,128)} async-done(((f32[32,1024]{1,0:T(8,128)}), f32[32,8192]{1,0:T(8,128)}) %all-gather.2.cloned.1.call-update) | async-done | bytes 1048592 | tf_op jit(solution)/shard_map/all_gather | solution.py:104
  189.3 8.0 %convolution_subtract_fusion = f32[128,8192]{1,0:T(8,128)} fusion(f32[128,8192]{1,0:T(8,128)} %param.4, f32[32,8192]{1,0:T(8,128)} %all-gather.2.cloned.1.call-done, f32[1024,32]{0,1:T(8,128)S(1)} %all_gather.6, s32[]{:T(128)S(6)} %select_n.3), kind=kOutput, calls=%fused_computation | convolution fusion | flops 403701760 | bytes 9453572 | tf_op jit(solution)/shard_map/dot_general | solution.py:102
  (922 shorter events, 30.0 us)
Async XLA Ops:
  12.1 6.6 %copy-start.56 = (s32[16]{0:T(128)S(1)}, s32[16]{0:T(128)}, u32[]{:S(2)}) copy-start(s32[16]{0:T(128)} %param.6) | copy-start | bytes 196
  12.1 6.7 %copy-start.17 = (f32[256,32]{0,1:T(8,128)S(1)}, f32[256,32]{0,1:T(8,128)}, u32[]{:S(2)}) copy-start(f32[256,32]{0,1:T(8,128)} %param.7) | copy-start | bytes 98308
  12.1 15.2 %copy-start = (s32[1024,512]{1,0:T(8,128)S(1)}, s32[1024,512]{1,0:T(8,128)}, u32[]{:S(2)}) copy-start(s32[1024,512]{1,0:T(8,128)} %param.5) | copy-start | bytes 6291460
  12.1 100.6 %all-to-all-start = ((f32[128,8,1024]{0,2,1:T(8,128)}), f32[128,8,1024]{0,2,1:T(8,128)}, u32[]{:S(2)}, u32[]{:S(2)}) async-start(f32[128,8,1024]{0,2,1:T(8,128)} %bitcast.362), calls=%async_computation | async-start | bytes 8388608 | tf_op jit(solution)/shard_map/all_to_all | solution.py:92
  18.6 170.7 %all-gather.2.cloned.1.call-start = ((), (), s32[]{:S(2)}) async-start(), calls=%async_computation.1 | async-start | bytes 1179648 | tf_op jit(solution)/shard_map/all_gather | solution.py:104
  44.0 82.0 %copy-start.19 = (f32[1,512]{1,0:T(1,128)}, f32[1,512]{1,0:T(1,128)S(1)}, u32[]{:S(2)}) copy-start(f32[1,512]{1,0:T(1,128)S(1)} %slice.1010) | copy-start | bytes 6148
  44.0 82.1 %copy-start.21 = (f32[1,512]{1,0:T(1,128)}, f32[1,512]{1,0:T(1,128)S(1)}, u32[]{:S(2)}) copy-start(f32[1,512]{1,0:T(1,128)S(1)} %slice.1017) | copy-start | bytes 6148
  44.0 82.2 %copy-start.23 = (f32[1,512]{1,0:T(1,128)}, f32[1,512]{1,0:T(1,128)S(1)}, u32[]{:S(2)}) copy-start(f32[1,512]{1,0:T(1,128)S(1)} %slice.1024) | copy-start | bytes 6148
  44.0 82.3 %copy-start.25 = (f32[1,512]{1,0:T(1,128)}, f32[1,512]{1,0:T(1,128)S(1)}, u32[]{:S(2)}) copy-start(f32[1,512]{1,0:T(1,128)S(1)} %slice.1031) | copy-start | bytes 6148
  44.1 82.4 %copy-start.27 = (f32[1,512]{1,0:T(1,128)}, f32[1,512]{1,0:T(1,128)S(1)}, u32[]{:S(2)}) copy-start(f32[1,512]{1,0:T(1,128)S(1)} %slice.1038) | copy-start | bytes 6148
  44.1 82.5 %copy-start.29 = (f32[1,512]{1,0:T(1,128)}, f32[1,512]{1,0:T(1,128)S(1)}, u32[]{:S(2)}) copy-start(f32[1,512]{1,0:T(1,128)S(1)} %slice.1045) | copy-start | bytes 6148
  44.1 82.6 %copy-start.31 = (f32[1,512]{1,0:T(1,128)}, f32[1,512]{1,0:T(1,128)S(1)}, u32[]{:S(2)}) copy-start(f32[1,512]{1,0:T(1,128)S(1)} %slice.1052) | copy-start | bytes 6148
  44.1 82.7 %copy-start.33 = (f32[1,512]{1,0:T(1,128)}, f32[1,512]{1,0:T(1,128)S(1)}, u32[]{:S(2)}) copy-start(f32[1,512]{1,0:T(1,128)S(1)} %slice.1059) | copy-start | bytes 6148
  44.1 82.8 %copy-start.34 = (f32[1,512]{1,0:T(1,128)}, f32[1,512]{1,0:T(1,128)S(1)}, u32[]{:S(2)}) copy-start(f32[1,512]{1,0:T(1,128)S(1)} %slice.1066) | copy-start | bytes 6148
  44.2 82.8 %copy-start.35 = (f32[1,512]{1,0:T(1,128)}, f32[1,512]{1,0:T(1,128)S(1)}, u32[]{:S(2)}) copy-start(f32[1,512]{1,0:T(1,128)S(1)} %slice.1073) | copy-start | bytes 6148
  44.2 82.9 %copy-start.36 = (f32[1,512]{1,0:T(1,128)}, f32[1,512]{1,0:T(1,128)S(1)}, u32[]{:S(2)}) copy-start(f32[1,512]{1,0:T(1,128)S(1)} %slice.1080) | copy-start | bytes 6148
  44.2 82.9 %copy-start.37 = (f32[1,512]{1,0:T(1,128)}, f32[1,512]{1,0:T(1,128)S(1)}, u32[]{:S(2)}) copy-start(f32[1,512]{1,0:T(1,128)S(1)} %slice.1087) | copy-start | bytes 6148
  44.2 83.0 %copy-start.38 = (f32[1,512]{1,0:T(1,128)}, f32[1,512]{1,0:T(1,128)S(1)}, u32[]{:S(2)}) copy-start(f32[1,512]{1,0:T(1,128)S(1)} %slice.1094) | copy-start | bytes 6148
  44.2 83.0 %copy-start.39 = (f32[1,512]{1,0:T(1,128)}, f32[1,512]{1,0:T(1,128)S(1)}, u32[]{:S(2)}) copy-start(f32[1,512]{1,0:T(1,128)S(1)} %slice.1101) | copy-start | bytes 6148
  44.3 83.1 %copy-start.40 = (f32[1,512]{1,0:T(1,128)}, f32[1,512]{1,0:T(1,128)S(1)}, u32[]{:S(2)}) copy-start(f32[1,512]{1,0:T(1,128)S(1)} %slice.1108) | copy-start | bytes 6148
  44.3 83.2 %copy-start.41 = (f32[1,512]{1,0:T(1,128)}, f32[1,512]{1,0:T(1,128)S(1)}, u32[]{:S(2)}) copy-start(f32[1,512]{1,0:T(1,128)S(1)} %slice.1115) | copy-start | bytes 6148
  52.1 3.9 %copy-start.9 = (f32[3,3,512]{2,1,0:T(4,128)}, f32[3,3,512]{2,1,0:T(4,128)S(1)}, u32[]{:S(2)}) copy-start(f32[3,3,512]{2,1,0:T(4,128)S(1)} %slice_subtract_fusion.52) | copy-start | bytes 55300
  126.3 1.5 copy-start.46
  126.4 1.5 copy-start.48
  126.5 1.5 copy-start.49
  126.5 1.5 copy-start.50
  126.5 1.6 copy-start.51
  126.5 1.6 copy-start.52
  126.6 1.6 copy-start.53
  126.6 1.6 copy-start.54
  126.6 1.6 copy-start.55
  127.6 1.6 copy-start.1
  127.7 1.5 copy-start.2
  134.9 18.7 %copy-start.42 = (f32[1,512]{1,0:T(1,128)S(1)}, f32[1,512]{1,0:T(1,128)}, u32[]{:S(2)}) copy-start(f32[1,512]{1,0:T(1,128)} %copy-done.41) | copy-start | bytes 6148
  150.6 11.4 %copy-start.32 = (f32[1,512]{1,0:T(1,128)S(1)}, f32[1,512]{1,0:T(1,128)}, u32[]{:S(2)}) copy-start(f32[1,512]{1,0:T(1,128)} %copy-done.31) | copy-start | bytes 6148
  152.4 10.1 %copy-start.30 = (f32[1,512]{1,0:T(1,128)S(1)}, f32[1,512]{1,0:T(1,128)}, u32[]{:S(2)}) copy-start(f32[1,512]{1,0:T(1,128)} %copy-done.29) | copy-start | bytes 6148
  153.6 9.4 %copy-start.28 = (f32[1,512]{1,0:T(1,128)S(1)}, f32[1,512]{1,0:T(1,128)}, u32[]{:S(2)}) copy-start(f32[1,512]{1,0:T(1,128)} %copy-done.27) | copy-start | bytes 6148
  154.8 8.7 %copy-start.26 = (f32[1,512]{1,0:T(1,128)S(1)}, f32[1,512]{1,0:T(1,128)}, u32[]{:S(2)}) copy-start(f32[1,512]{1,0:T(1,128)} %copy-done.25) | copy-start | bytes 6148
  156.6 7.3 %copy-start.24 = (f32[1,512]{1,0:T(1,128)S(1)}, f32[1,512]{1,0:T(1,128)}, u32[]{:S(2)}) copy-start(f32[1,512]{1,0:T(1,128)} %copy-done.23) | copy-start | bytes 6148
  157.8 6.7 %copy-start.22 = (f32[1,512]{1,0:T(1,128)S(1)}, f32[1,512]{1,0:T(1,128)}, u32[]{:S(2)}) copy-start(f32[1,512]{1,0:T(1,128)} %copy-done.21) | copy-start | bytes 6148
  158.9 6.1 %copy-start.20 = (f32[1,512]{1,0:T(1,128)S(1)}, f32[1,512]{1,0:T(1,128)}, u32[]{:S(2)}) copy-start(f32[1,512]{1,0:T(1,128)} %copy-done.19) | copy-start | bytes 6148
  160.8 4.9 %copy-start.18 = (f32[16,32]{1,0:T(8,128)S(1)}, f32[16,32]{1,0:T(8,128)}, u32[]{:S(2)}) copy-start(f32[16,32]{1,0:T(8,128)} %div.867) | copy-start | bytes 6148
  162.3 3.6 %copy-start.16 = (f32[1,2,16,32]{3,2,1,0:T(8,128)S(1)}, f32[1,2,16,32]{3,2,1,0:T(8,128)}, u32[]{:S(2)}) copy-start(f32[1,2,16,32]{3,2,1,0:T(8,128)} %stack.177) | copy-start | bytes 12292
  162.4 3.6 %copy-start.15 = (f32[1,2,16,32]{3,2,1,0:T(8,128)S(1)}, f32[1,2,16,32]{3,2,1,0:T(8,128)}, u32[]{:S(2)}) copy-start(f32[1,2,16,32]{3,2,1,0:T(8,128)} %stack.178) | copy-start | bytes 12292
  162.4 3.6 %copy-start.14 = (f32[1,2,16,32]{3,2,1,0:T(8,128)S(1)}, f32[1,2,16,32]{3,2,1,0:T(8,128)}, u32[]{:S(2)}) copy-start(f32[1,2,16,32]{3,2,1,0:T(8,128)} %stack.179) | copy-start | bytes 12292
  162.5 3.7 %copy-start.13 = (f32[1,2,16,32]{3,2,1,0:T(8,128)S(1)}, f32[1,2,16,32]{3,2,1,0:T(8,128)}, u32[]{:S(2)}) copy-start(f32[1,2,16,32]{3,2,1,0:T(8,128)} %stack.182) | copy-start | bytes 12292
  162.5 3.8 %copy-start.12 = (f32[1,2,16,32]{3,2,1,0:T(8,128)S(1)}, f32[1,2,16,32]{3,2,1,0:T(8,128)}, u32[]{:S(2)}) copy-start(f32[1,2,16,32]{3,2,1,0:T(8,128)} %stack.183) | copy-start | bytes 12292
  162.5 3.7 %copy-start.11 = (f32[1,2,16,32]{3,2,1,0:T(8,128)S(1)}, f32[1,2,16,32]{3,2,1,0:T(8,128)}, u32[]{:S(2)}) copy-start(f32[1,2,16,32]{3,2,1,0:T(8,128)} %stack.184) | copy-start | bytes 12292
  (11 other events, 14.4 us)
Sparse Core Ops, SparseCore 0:
  168.1 21.1 all-gather.1
where the time goes:
time: 205 us; the launch traced here: 204 us
  waiting for transfers between devices  72.7 us (35%)
  local copies, waits for them, and re-layouts  49.4 us (24%)
  other arithmetic  32.3 us (16%)
  between operations  17.4 us (8%)
  matrix products  17.3 us (8%)
  blocking collectives  8.45 us (4%)
  starting transfers between devices  6.53 us (3%)
    all_to_all x1, waiting for transfers between devices, per_device(): lax.all_to_all(visibility, 'chan', split_axis=1, concat_axis=0, tiled=True)  51.3 us
    all_gather x1, waiting for transfers between devices, per_device(): lax.all_gather(mode_amplitudes, 'chan', axis=1, tiled=True)  21.3 us
    unnamed x578, local copies, waits for them, and re-layouts  16.9 us
    unnamed x28, other arithmetic  14.1 us
    all_gather x1, blocking collectives, per_device(): spectral_templates = lax.all_gather(fit_modes, 'grp', axis=0, tiled=True)  8.45 us
    dot_general x1, matrix products, per_device(): jnp.dot(local_basis, lax.all_gather(mode_amplitudes, 'chan', axis=1, tile...  8 us
    mul x2, local copies, waits for them, and re-layouts, solve_amplitudes(): assigned_rows.reshape(channel_count, antenna_pairs_list, 2, sample_values)  7.88 us
    slice x32, local copies, waits for them, and re-layouts, solve_normal(): current = remains[0] / column[0][None, :]  7.51 us
  transfers between devices with their start and end apart: 2, of which 2 were waited for; matrix products, arithmetic and copies ran while one was open for 16% of the time, Pallas kernels for 0%

commit v1 on v0

--- a/solution.py
+++ b/solution.py
@@ -89,7 +89,12 @@
 
 def per_device(visibility, interference_mask, valid_time_count, fit_modes):
     spectral_templates = lax.all_gather(fit_modes, "grp", axis=0, tiled=True)
-    assigned_rows = lax.all_to_all(visibility, "chan", split_axis=1, concat_axis=0, tiled=True)
+    assigned_rows = jnp.concatenate(
+        lax.all_to_all(
+            jnp.stack(jnp.split(visibility, lax.axis_size("chan"), axis=1)), "chan", 0, 0
+        ),
+        axis=0,
+    )
     antenna_pairs_list = valid_time_count.shape[0]
     sample_weight = fit_weight(interference_mask, valid_time_count)
     mode_amplitudes = solve_amplitudes(

time: 205 us -> 249 us (1.21)
  local copies, waits for them, and re-layouts: 49.4 us -> 87.9 us
  other arithmetic: 32.3 us -> 38.9 us
  waiting for transfers between devices: 72.7 us -> 69.5 us
    unnamed x578 -> x622, local copies, waits for them, and re-layouts: 16.9 us -> 49.5 us
    slice x32, local copies, waits for them, and re-layouts: 7.51 us -> 17.5 us  [solve_normal(): current = remains[0] / column[0][None, :]]
    mul x2 -> x0, local copies, waits for them, and re-layouts: 7.88 us -> none  [solve_amplitudes(): assigned_rows.reshape(channel_count, antenna_pairs_list, 2, sample_values)]
    another operation x0 -> x2, local copies, waits for them, and re-layouts: none -> 7.22 us  [the longest x1 5.34 us: solve_amplitudes(): assigned_rows.reshape(channel_count, antenna_pairs_list, 2, sample_values)]
    all_to_all x1 -> x0, local copies, waits for them, and re-layouts: 5.34 us -> none  [per_device(): lax.all_to_all(visibility, 'chan', split_axis=1, concat_axis=0, tiled=True)]
    unnamed x28, other arithmetic: 14.1 us -> 18.6 us
    reduce_sum x30, other arithmetic: 3.05 us -> 6.94 us  [solve_normal(): current = current - jnp.sum(column[1:, None, :] * later_rows, axis=0)]
    all_to_all x1, waiting for transfers between devices: 51.3 us -> 48.2 us  [per_device(): lax.all_to_all(jnp.stack(jnp.split(visibility, lax.axis_size('chan'), axi...]
  transfers between devices with their start and end apart: 2 -> 2, of which waited for: 2 -> 2; matrix products, arithmetic and copies ran while one was open for 16% -> 14% of each run, Pallas kernels for 0% -> 0%
where the time goes in v1:
time: 249 us; the launch traced here: 247 us
  local copies, waits for them, and re-layouts  87.9 us (35%)
  waiting for transfers between devices  69.5 us (28%)
  other arithmetic  38.9 us (16%)
  matrix products  18.7 us (8%)
  between operations  17.5 us (7%)
  blocking collectives  8.45 us (3%)
  starting transfers between devices  6.52 us (3%)
    unnamed x622, local copies, waits for them, and re-layouts  49.5 us
    all_to_all x1, waiting for transfers between devices, per_device(): lax.all_to_all(jnp.stack(jnp.split(visibility, lax.axis_size('chan'), axi...  48.2 us
    all_gather x1, waiting for transfers between devices, per_device(): lax.all_gather(mode_amplitudes, 'chan', axis=1, tiled=True)  21.3 us
    unnamed x28, other arithmetic  18.6 us
    slice x32, local copies, waits for them, and re-layouts, solve_normal(): current = remains[0] / column[0][None, :]  17.5 us
    all_gather x1, blocking collectives, per_device(): spectral_templates = lax.all_gather(fit_modes, 'grp', axis=0, tiled=True)  8.45 us
    dot_general x1, matrix products, per_device(): jnp.dot(local_basis, lax.all_gather(mode_amplitudes, 'chan', axis=1, tile...  8.01 us
    reduce_sum x30, other arithmetic, solve_normal(): current = current - jnp.sum(column[1:, None, :] * later_rows, axis=0)  6.94 us
  transfers between devices with their start and end apart: 2, of which 2 were waited for; matrix products, arithmetic and copies ran while one was open for 14% of the time, Pallas kernels for 0%

profile of v1, /device:TPU:0, one launch (start us, length us, event | category | flops | bytes accessed | tf_op | source)
XLA Modules:
  0.0 247.4 jit_solution(5202021273358835567)
XLA Ops:
  6.5 1.9 constant_dynamic-update-slice_fusion.7
  8.4 1.9 constant_dynamic-update-slice_fusion.6
  10.3 1.9 constant_dynamic-update-slice_fusion.5
  12.2 1.9 constant_dynamic-update-slice_fusion.4
  14.1 1.9 constant_dynamic-update-slice_fusion.3
  16.0 1.9 constant_dynamic-update-slice_fusion.2
  17.8 1.9 constant_dynamic-update-slice_fusion.1
  19.7 1.9 constant_dynamic-update-slice_fusion
  21.6 6.5 %all-to-all-start = ((f32[8,128,1024]{2,1,0:T(8,128)}), f32[8,128,1024]{2,1,0:T(8,128)}, u32[]{:S(2)}, u32[]{:S(2)}) async-start(f32[8,128,1024]{2,1,0:T(8,128)} %constant_dynamic-update-slice_fusion), calls=%async_computation | async-start | bytes 8388608 | tf_op jit(solution)/shard_map/all_to_all | solution.py:93
  28.3 8.5 %all_gather.6 = f32[1024,32]{0,1:T(8,128)S(1)} all-gather(f32[256,32]{0,1:T(8,128)S(1)} %copy-done.38), channel_id=1, replica_groups=mesh['grp'=4,'chan'=8] {'grp'}, dimensions={0}, use_global_device_ids=true | all-gather | bytes 163840 | tf_op jit(solution)/shard_map/all_gather | solution.py:91
  36.8 1.9 copy.42
  38.7 1.8 subtract_multiply_fusion
  40.5 6.7 %fusion.6 = f32[32,32,512]{2,1,0:T(8,128)S(1)} fusion(f32[1024,512]{0,1:T(8,128)S(1)} %subtract_multiply_fusion, f32[1024,32]{0,1:T(8,128)S(1)} %all_gather.6, f32[32,32]{1,0:T(8,128)S(1)} %fusion.13), kind=kOutput, calls=%fused_computation.16 | convolution fusion | flops 6444023808 | bytes 4329472 | tf_op jit(solution)/shard_map/dot_general | solution.py:53
  74.0 48.2 %all-to-all-done = f32[8,128,1024]{2,1,0:T(8,128)} async-done(((f32[8,128,1024]{2,1,0:T(8,128)}), f32[8,128,1024]{2,1,0:T(8,128)}, u32[]{:S(2)}, u32[]{:S(2)}) %all-to-all-start) | async-done | bytes 4194336 | tf_op jit(solution)/shard_map/all_to_all | solution.py:93
  122.2 5.3 %copy.47 = f32[1024,1024]{0,1:T(8,128)} copy(f32[1024,1024]{1,0:T(8,128)} %bitcast.8) | data formatting | bytes 8388608 | tf_op jit(solution)/shard_map/reshape;reshape | solution.py:66
  127.6 2.7 %bitcast_multiply_fusion = f32[1024,1024]{0,1:T(8,128)S(1)} fusion(f32[1024,1024]{0,1:T(8,128)} %copy.47, f32[1024,16,32]{0,2,1:T(8,128)S(1)} %bitcast.376), kind=kLoop, calls=%fused_computation.3 | loop fusion | flops 1048576 | bytes 10485760 | tf_op jit(solution)/shard_map/mul | solution.py:66
  130.3 3.9 %convolution_bitcast_fusion = f32[32,1024]{1,0:T(8,128)S(1)} fusion(f32[1024,1024]{0,1:T(8,128)S(1)} %bitcast_multiply_fusion, f32[1024,32]{0,1:T(8,128)S(1)} %copy-done.18), kind=kOutput, calls=%fused_computation.18 | convolution fusion | flops 402653184 | bytes 4456448 | tf_op jit(solution)/shard_map/dot_general | solution.py:70
  137.9 0.7 slice_subtract_fusion.58
  138.8 0.7 stack.211
  140.2 0.7 fusion.46
  140.9 0.7 stack.209
  141.6 0.7 fusion.45
  143.0 0.7 constant_dynamic-update-slice_fusion.12
  143.7 1.3 constant_dynamic-update-slice_fusion.18
  148.1 0.8 multiply_reduce_fusion.25
  148.9 1.3 constant_dynamic-update-slice_fusion.25
  150.1 0.7 stack.206
  154.4 0.8 multiply_reduce_fusion.24
  155.1 1.3 constant_dynamic-update-slice_fusion.33
  160.6 0.8 multiply_reduce_fusion.23
  161.4 1.3 constant_dynamic-update-slice_fusion.42
  167.5 0.8 multiply_reduce_fusion.22
  168.3 1.3 constant_dynamic-update-slice_fusion.52
  175.0 0.8 multiply_reduce_fusion.21
  175.8 1.3 constant_dynamic-update-slice_fusion.63
  183.1 0.8 multiply_reduce_fusion.20
  183.9 1.3 constant_dynamic-update-slice_fusion.75
  191.8 0.8 multiply_reduce_fusion.19
  192.6 0.7 constant_dynamic-update-slice_fusion.88
  196.4 0.7 constant_dynamic-update-slice_fusion.150
  197.4 0.7 constant_dynamic-update-slice_fusion.168
  198.4 0.7 constant_dynamic-update-slice_fusion.187
  199.5 0.7 constant_dynamic-update-slice_fusion.207
  200.5 0.7 constant_dynamic-update-slice_fusion.228
  204.7 0.7 constant_dynamic-update-slice_fusion.322
  209.9 1.3 reshape.1015
  211.3 21.3 %all-gather.2.cloned.1.call-done = f32[32,8192]{1,0:T(8,128)} async-done(((f32[32,1024]{1,0:T(8,128)}), f32[32,8192]{1,0:T(8,128)}) %all-gather.2.cloned.1.call-update) | async-done | bytes 1048592 | tf_op jit(solution)/shard_map/all_gather | solution.py:109
  232.6 8.0 %convolution_subtract_fusion = f32[128,8192]{1,0:T(8,128)} fusion(f32[128,8192]{1,0:T(8,128)} %param.4, f32[32,8192]{1,0:T(8,128)} %all-gather.2.cloned.1.call-done, f32[1024,32]{0,1:T(8,128)} %copy-done.17, s32[]{:T(128)S(6)} %select_n.3), kind=kOutput, calls=%fused_computation | convolution fusion | flops 403701760 | bytes 9453572 | tf_op jit(solution)/shard_map/dot_general | solution.py:107
  (965 shorter events, 74.5 us)
Async XLA Ops:
  21.6 6.6 %copy-start.75 = (s32[16]{0:T(128)S(1)}, s32[16]{0:T(128)}, u32[]{:S(2)}) copy-start(s32[16]{0:T(128)} %param.6) | copy-start | bytes 196
  21.6 6.7 %copy-start.38 = (f32[256,32]{0,1:T(8,128)S(1)}, f32[256,32]{0,1:T(8,128)}, u32[]{:S(2)}) copy-start(f32[256,32]{0,1:T(8,128)} %param.7) | copy-start | bytes 98308
  21.6 15.2 %copy-start = (s32[1024,512]{1,0:T(8,128)S(1)}, s32[1024,512]{1,0:T(8,128)}, u32[]{:S(2)}) copy-start(s32[1024,512]{1,0:T(8,128)} %param.5) | copy-start | bytes 6291460
  21.6 100.6 %all-to-all-start = ((f32[8,128,1024]{2,1,0:T(8,128)}), f32[8,128,1024]{2,1,0:T(8,128)}, u32[]{:S(2)}, u32[]{:S(2)}) async-start(f32[8,128,1024]{2,1,0:T(8,128)} %constant_dynamic-update-slice_fusion), calls=%async_computation | async-start | bytes 8388608 | tf_op jit(solution)/shard_map/all_to_all | solution.py:93
  28.1 204.5 %all-gather.2.cloned.1.call-start = ((), (), s32[]{:S(2)}) async-start(), calls=%async_computation.1 | async-start | bytes 1179648 | tf_op jit(solution)/shard_map/all_gather | solution.py:109
  36.8 3.7 %copy-start.17 = (f32[1024,32]{0,1:T(8,128)}, f32[1024,32]{0,1:T(8,128)S(1)}, u32[]{:S(2)}) copy-start(f32[1024,32]{0,1:T(8,128)S(1)} %all_gather.6) | copy-start | bytes 393220
  54.7 13.4 %copy-start.1 = (f32[13,512]{1,0:T(8,128)}, f32[13,512]{1,0:T(8,128)S(1)}, u32[]{:S(2)}) copy-start(f32[13,512]{1,0:T(8,128)S(1)} %slice.1130) | copy-start | bytes 79876
  66.6 5.4 %copy-start.9 = (f32[11,512]{1,0:T(8,128)}, f32[11,512]{1,0:T(8,128)S(1)}, u32[]{:S(2)}) copy-start(f32[11,512]{1,0:T(8,128)S(1)} %slice.1144) | copy-start | bytes 67588
  67.4 60.2 %copy-start.13 = (f32[10,512]{1,0:T(8,128)}, f32[10,512]{1,0:T(8,128)S(1)}, u32[]{:S(2)}) copy-start(f32[10,512]{1,0:T(8,128)S(1)} %slice.1151) | copy-start | bytes 61444
  68.1 59.5 %copy-start.5 = (f32[9,512]{1,0:T(8,128)}, f32[9,512]{1,0:T(8,128)S(1)}, u32[]{:S(2)}) copy-start(f32[9,512]{1,0:T(8,128)S(1)} %slice.1158) | copy-start | bytes 55300
  70.6 67.0 %copy-start.19 = (f32[6,512]{1,0:T(8,128)}, f32[6,512]{1,0:T(8,128)S(1)}, u32[]{:S(2)}) copy-start(f32[6,512]{1,0:T(8,128)S(1)} %slice.1179) | copy-start | bytes 36868
  71.3 56.2 %copy-start.22 = (f32[5,512]{1,0:T(8,128)}, f32[5,512]{1,0:T(8,128)S(1)}, u32[]{:S(2)}) copy-start(f32[5,512]{1,0:T(8,128)S(1)} %slice.1186) | copy-start | bytes 30724
  72.7 54.8 %copy-start.31 = (f32[3,3,512]{2,1,0:T(4,128)}, f32[3,3,512]{2,1,0:T(4,128)S(1)}, u32[]{:S(2)}) copy-start(f32[3,3,512]{2,1,0:T(4,128)S(1)} %slice_subtract_fusion.52) | copy-start | bytes 55300
  127.5 2.8 %copy-start.18 = (f32[1024,32]{0,1:T(8,128)S(1)}, f32[1024,32]{0,1:T(8,128)}, u32[]{:S(2)}) copy-start(f32[1024,32]{0,1:T(8,128)} %copy-done.17) | copy-start | bytes 393220
  134.9 1.6 copy-start.55
  134.9 1.7 copy-start.56
  135.0 1.7 copy-start.57
  135.3 1.6 copy-start.60
  135.5 1.6 copy-start.62
  135.5 1.6 copy-start.63
  135.6 1.6 copy-start.12
  135.6 1.6 copy-start.64
  135.6 1.7 copy-start.10
  135.7 1.6 copy-start.65
  135.7 1.6 copy-start.14
  135.7 1.7 copy-start.66
  135.7 1.7 copy-start.6
  135.8 1.6 copy-start.67
  135.8 1.7 copy-start.68
  135.9 1.7 copy-start.21
  135.9 1.7 copy-start.69
  136.0 1.7 copy-start.70
  136.0 1.7 copy-start.23
  136.0 1.8 copy-start.71
  136.0 1.8 copy-start.72
  136.0 1.8 copy-start.73
  137.7 1.8 copy-start.29
  193.4 12.5 %copy-start.50 = (f32[1,512]{1,0:T(1,128)S(1)}, f32[1,512]{1,0:T(1,128)}, u32[]{:S(2)}) copy-start(f32[1,512]{1,0:T(1,128)} %slice.1045) | copy-start | bytes 6148
  195.2 11.2 %copy-start.48 = (f32[1,512]{1,0:T(1,128)S(1)}, f32[1,512]{1,0:T(1,128)}, u32[]{:S(2)}) copy-start(f32[1,512]{1,0:T(1,128)} %slice.1038) | copy-start | bytes 6148
  196.4 10.5 %copy-start.46 = (f32[1,512]{1,0:T(1,128)S(1)}, f32[1,512]{1,0:T(1,128)}, u32[]{:S(2)}) copy-start(f32[1,512]{1,0:T(1,128)} %slice.1031) | copy-start | bytes 6148
  198.2 9.1 %copy-start.44 = (f32[1,512]{1,0:T(1,128)S(1)}, f32[1,512]{1,0:T(1,128)}, u32[]{:S(2)}) copy-start(f32[1,512]{1,0:T(1,128)} %slice.1024) | copy-start | bytes 6148
  199.4 8.4 %copy-start.42 = (f32[1,512]{1,0:T(1,128)S(1)}, f32[1,512]{1,0:T(1,128)}, u32[]{:S(2)}) copy-start(f32[1,512]{1,0:T(1,128)} %slice.1017) | copy-start | bytes 6148
  201.3 7.1 %copy-start.40 = (f32[1,512]{1,0:T(1,128)S(1)}, f32[1,512]{1,0:T(1,128)}, u32[]{:S(2)}) copy-start(f32[1,512]{1,0:T(1,128)} %slice.1010) | copy-start | bytes 6148
  204.7 4.8 %copy-start.37 = (f32[1,2,16,32]{3,2,1,0:T(8,128)S(1)}, f32[1,2,16,32]{3,2,1,0:T(8,128)}, u32[]{:S(2)}) copy-start(f32[1,2,16,32]{3,2,1,0:T(8,128)} %stack.206) | copy-start | bytes 12292
  205.5 4.0 %copy-start.36 = (f32[1,2,16,32]{3,2,1,0:T(8,128)S(1)}, f32[1,2,16,32]{3,2,1,0:T(8,128)}, u32[]{:S(2)}) copy-start(f32[1,2,16,32]{3,2,1,0:T(8,128)} %stack.208) | copy-start | bytes 12292
  205.6 4.0 %copy-start.35 = (f32[1,2,16,32]{3,2,1,0:T(8,128)S(1)}, f32[1,2,16,32]{3,2,1,0:T(8,128)}, u32[]{:S(2)}) copy-start(f32[1,2,16,32]{3,2,1,0:T(8,128)} %stack.209) | copy-start | bytes 12292
  205.6 3.9 %copy-start.34 = (f32[1,2,16,32]{3,2,1,0:T(8,128)S(1)}, f32[1,2,16,32]{3,2,1,0:T(8,128)}, u32[]{:S(2)}) copy-start(f32[1,2,16,32]{3,2,1,0:T(8,128)} %stack.210) | copy-start | bytes 12292
  205.7 3.9 %copy-start.33 = (f32[1,2,16,32]{3,2,1,0:T(8,128)S(1)}, f32[1,2,16,32]{3,2,1,0:T(8,128)}, u32[]{:S(2)}) copy-start(f32[1,2,16,32]{3,2,1,0:T(8,128)} %stack.211) | copy-start | bytes 12292
  (30 other events, 37.3 us)
Sparse Core Ops, SparseCore 0:
  211.4 21.1 all-gather.1
